TPU v7x, 32 devices: a whole 2x2x4 slice. The times are simulated.
32 devices in a mesh: ctx: 8 (over z, core), tp: 4 (over y, x).
Axes of the slice: x: 2, y: 2, z: 4, core: 2. Of those that a mesh axis runs over, the one named last changes fastest.
Arguments:
- tokens: bfloat16 [2, 4096, 8192], P(None, 'ctx', 'tp'), may hold values from -14 to 14
- norm_gain: float32 [8192], replicated, may hold values from 0.5 to 1.5
- span_order: int32 [2, 16], replicated, may hold values from 0 to 15, each once within a row
- w_query: bfloat16 [8192, 4096], P('ctx', 'tp'), may hold values from -0.10122281 to 0.10122281
- w_key: bfloat16 [8192, 1024], P('ctx', 'tp'), may hold values from -0.10122281 to 0.10122281
- value_weight: bfloat16 [8192, 1024], P('ctx', 'tp'), may hold values from -0.0625 to 0.0625
- w_out: bfloat16 [4096, 8192], P('tp', 'ctx'), may hold values from -0.75 to 0.75
Outputs:
- mixed: bfloat16 [2, 4096, 8192], P(None, 'ctx', 'tp')
Inputs may be any that keep to these rules, and one draw needn't show every extreme that they name: Each row of span_order names every one of the 2 * 8 blocks of positions once; stored block b of a sequence holds positions span_order[b] * 256 onwards, in order.
All inputs are finite; a program needn't handle non-finite values.
Results may differ from a plain program's by a relative error of at most 0.014.
Values may be sent and summed in bfloat16 or wider, within the bound.
A program may use at most 128 MiB of HBM per device.

v0:
```python
import math
import jax
import jax.numpy as jnp
from jax import lax
from jax.sharding import PartitionSpec as P

HEAD_DIM = 128
theta_base = 500000.0
norm_eps = 1e-05
masked_score = -1e30


def normalize(flat_rows, norm_gain):
    wide = flat_rows.astype(jnp.float32)
    factor = lax.rsqrt(jnp.mean(wide * wide, axis=-1, keepdims=True) + norm_eps)
    return (wide * factor * norm_gain).astype(jnp.bfloat16)


def positions_of(span_order, first, count, block_rows):
    stored = first + jnp.arange(count, dtype=jnp.int32)
    which = stored // block_rows
    slots = jnp.arange(span_order.shape[1], dtype=jnp.int32)
    picked = jnp.sum(
        jnp.where(slots[None, None, :] == which[None, :, None], span_order[:, None, :], 0), axis=2
    )
    return picked * block_rows + stored % block_rows


def apply_rotation(value_rows, token_position, head_size):
    half = head_size // 2
    freqs = jnp.exp(-(2.0 * jnp.arange(half, dtype=jnp.float32) / head_size) * math.log(theta_base))
    angle = token_position.astype(jnp.float32)[..., None] * freqs
    cosine = jnp.cos(angle)[:, :, None, :]
    sine = jnp.sin(angle)[:, :, None, :]
    front = value_rows[..., :half]
    back = value_rows[..., half:]
    return jnp.concatenate([front * cosine - back * sine, back * cosine + front * sine], axis=-1)


def per_device(tokens, norm_gain, span_order, w_query, w_key, value_weight, w_out):
    sequence_batch, rows_dev, _ = tokens.shape
    head_size = HEAD_DIM
    query_heads = w_query.shape[1] // head_size
    key_heads = w_key.shape[1] // head_size
    group_width = query_heads // key_heads
    block_rows = rows_dev // 2
    total_rows = sequence_batch * rows_dev
    factor = 1.0 / math.sqrt(head_size)
    rank = lax.axis_index("ctx")
    whole = lax.all_gather(tokens, "tp", axis=2, tiled=True)
    normed = normalize(whole.reshape(total_rows, whole.shape[2]), norm_gain)
    query_pos = positions_of(span_order, rank * rows_dev, rows_dev, block_rows)
    latest = jnp.max(query_pos, axis=1)
    stat_shape = (sequence_batch, key_heads, group_width, rows_dev)
    initial = (
        jnp.full(stat_shape, masked_score, jnp.float32),
        jnp.zeros(stat_shape, jnp.float32),
        jnp.zeros(stat_shape + (head_size,), jnp.float32),
    )
    pieces = (
        lax.all_gather(w_query, "ctx", axis=0, tiled=True),
        lax.all_gather(w_key, "ctx", axis=0, tiled=True),
        lax.all_gather(value_weight, "ctx", axis=0, tiled=True),
    )
    query_flat, flattened_key, flattened_value = tuple(
        (jnp.dot(normed, piece, preferred_element_type=jnp.float32) for piece in pieces)
    )
    turned = apply_rotation(
        query_flat.reshape(sequence_batch, rows_dev, query_heads, head_size), query_pos, head_size
    ).astype(jnp.bfloat16)
    query = turned.reshape(sequence_batch, rows_dev, key_heads, group_width, head_size).transpose(
        0, 2, 3, 1, 4
    )
    turned = apply_rotation(
        flattened_key.reshape(sequence_batch, rows_dev, key_heads, head_size), query_pos, head_size
    ).astype(jnp.bfloat16)
    own_values = flattened_value.reshape(sequence_batch, rows_dev, key_heads, head_size).astype(
        jnp.bfloat16
    )
    key_piece = lax.all_gather(turned, "ctx", axis=1, tiled=True)
    value_piece = lax.all_gather(own_values, "ctx", axis=1, tiled=True)
    count = key_piece.shape[1]
    step_rows = 512

    def one_block(index, state):
        first = index * step_rows
        key_block = lax.dynamic_slice_in_dim(key_piece, first, step_rows, 1)
        value_block = lax.dynamic_slice_in_dim(value_piece, first, step_rows, 1)
        key_pos = positions_of(span_order, first, step_rows, block_rows)

        def update(current):
            peak, total, summed = current
            scores = (
                jnp.einsum(
                    "shgqd,skhd->shgqk", query, key_block, preferred_element_type=jnp.float32
                )
                * factor
            )
            allowed = key_pos[:, None, None, None, :] <= query_pos[:, None, None, :, None]
            scores = jnp.where(allowed, scores, masked_score)
            new_peak = jnp.maximum(peak, jnp.max(scores, axis=-1))
            weights = jnp.where(allowed, jnp.exp(scores - new_peak[..., None]), 0.0)
            shrink = jnp.exp(peak - new_peak)
            total = total * shrink + jnp.sum(weights, axis=-1)
            summed = summed * shrink[..., None] + jnp.einsum(
                "shgqk,skhd->shgqd",
                weights.astype(jnp.bfloat16),
                value_block,
                preferred_element_type=jnp.float32,
            )
            return (new_peak, total, summed)

        return lax.cond(
            jnp.all(jnp.min(key_pos, axis=1) > latest), lambda kept: kept, update, state
        )

    peak, total, summed = lax.fori_loop(0, count // step_rows, one_block, initial)
    attended = (summed / total[..., None]).astype(jnp.bfloat16)
    attended = attended.transpose(0, 3, 1, 2, 4).reshape(total_rows, query_heads * head_size)
    terms = jnp.dot(
        attended,
        lax.all_gather(w_out, "ctx", axis=1, tiled=True),
        preferred_element_type=jnp.float32,
    )
    mixed = lax.psum_scatter(terms.astype(jnp.bfloat16), "tp", scatter_dimension=1, tiled=True)
    return mixed.reshape(sequence_batch, rows_dev, mixed.shape[1])


def solution(mesh):
    placed = (
        P(None, "ctx", "tp"),
        P(),
        P(),
        P("ctx", "tp"),
        P("ctx", "tp"),
        P("ctx", "tp"),
        P("tp", "ctx"),
    )
    return jax.shard_map(
        per_device, mesh=mesh, in_specs=placed, out_specs=P(None, "ctx", "tp"), check_vma=False
    )
```

profile of v0, /device:TPU:0, one launch (start us, length us, event | category | flops | bytes accessed | tf_op | source)
XLA Modules:
  0.0 862.1 jit_solution(7252307660646929625)
XLA Ops:
  10.5 48.0 %all-gather.10.cloned.1.call-done = bf16[8192,256]{1,0:T(8,128)(2,1)} async-done(((bf16[1024,256]{1,0:T(8,128)(2,1)}), bf16[8192,256]{1,0:T(8,128)(2,1)}) %all-gather.10.cloned.1.call-update) | async-done | bytes 4194320 | tf_op jit(solution)/shard_map/all_gather | solution.py:62
  58.6 6.3 copy.24
  64.9 151.7 %all-gather.8.cloned.1.call-done = bf16[2,512,8192]{2,1,0:T(8,128)(2,1)} async-done(((bf16[2,512,2048]{2,1,0:T(8,128)(2,1)}), bf16[2,512,8192]{2,1,0:T(8,128)(2,1)}) %all-gather.8.cloned.1.call-update) | async-done | bytes 16777232 | tf_op jit(solution)/shard_map/all_gather | solution.py:50
  216.5 7.5 fusion.21
  224.0 9.0 %fusion.29 = f32[2,512,2,128]{1,3,2,0:T(8,128)S(1)} fusion(bf16[2,128,8192,1]{2,1,0,3:T(8,128)(2,1)S(1)} %bitcast.69, bf16[2,512,8192]{2,1,0:T(8,128)(2,1)} %all-gather.8.cloned.1.call-done, f32[8192]{0:T(1024)S(1)} %copy-done.2, f32[2,512]{1,0:T(2,128)S(1)} %add_rsqrt_fusion), kind=kOutput, calls=%fused_computation.49 | convolution fusion | flops 4328521728 | bytes 22056960 | tf_op jit(solution)/shard_map/dot_general | solution.py:66
  234.2 30.9 %all-gather.16.cloned.1.call-done = bf16[8192,256]{1,0:T(8,128)(2,1)} async-done(((bf16[1024,256]{1,0:T(8,128)(2,1)}), bf16[8192,256]{1,0:T(8,128)(2,1)}) %all-gather.16.cloned.1.call-update) | async-done | bytes 4194320 | tf_op jit(solution)/shard_map/all_gather | solution.py:63
  265.1 6.3 copy.28
  271.4 12.7 %convolution_convert_fusion.1 = bf16[2,512,2,128]{3,1,2,0:T(8,128)(2,1)} fusion(bf16[2,128,8192,1]{2,1,0,3:T(8,128)(2,1)} %bitcast.70, bf16[2,512,8192]{2,1,0:T(8,128)(2,1)} %all-gather.8.cloned.1.call-done, f32[8192]{0:T(1024)S(1)} %copy-done.2, f32[2,512]{1,0:T(2,128)S(1)} %add_rsqrt_fusion), kind=kOutput, calls=%fused_computation.47 | convolution fusion | flops 4328783872 | bytes 21532672 | tf_op jit(solution)/shard_map/dot_general | solution.py:66
  285.2 131.2 %all-gather.14.cloned.1.call-done = bf16[8192,1024]{1,0:T(8,128)(2,1)} async-done(((bf16[1024,1024]{1,0:T(8,128)(2,1)}), bf16[8192,1024]{1,0:T(8,128)(2,1)}) %all-gather.14.cloned.1.call-update) | async-done | bytes 16777232 | tf_op jit(solution)/shard_map/all_gather | solution.py:61
  416.4 21.4 %copy.25 = bf16[1024,8192]{1,0:T(8,128)(2,1)} copy(bf16[1024,8192]{0,1:T(8,128)(2,1)} %bitcast.63) | data formatting | bytes 33554432 | tf_op jit(solution)/shard_map/dot_general | solution.py:66
  437.9 22.4 %fusion.27 = f32[2,512,8,128]{1,3,2,0:T(8,128)S(1)} fusion(bf16[8,128,8192,1]{2,1,0,3:T(8,128)(2,1)} %bitcast.64, bf16[2,512,8192]{2,1,0:T(8,128)(2,1)} %all-gather.8.cloned.1.call-done, f32[8192]{0:T(1024)S(1)} %copy-done.2, f32[2,512]{1,0:T(2,128)S(1)} %add_rsqrt_fusion), kind=kOutput, calls=%fused_computation.48 | convolution fusion | flops 17213423616 | bytes 37785600 | tf_op jit(solution)/shard_map/dot_general | solution.py:66
  469.9 6.4 copy.29
  476.3 33.8 %all-gather.18.cloned.1.call-done = bf16[2,4096,2,128]{3,1,2,0:T(8,128)(2,1)} async-done(((bf16[2,512,2,128]{3,1,2,0:T(8,128)(2,1)}), bf16[2,4096,2,128]{3,1,2,0:T(8,128)(2,1)}) %all-gather.18.cloned.1.call-update) | async-done | bytes 4194320 | tf_op jit(solution)/shard_map/all_gather | solution.py:81
  512.6 156.1 %while.19 = (s32[]{:T(128)}, f32[2,2,4,512]{3,2,1,0:T(4,128)S(1)}, f32[2,2,4,512]{3,2,1,0:T(4,128)S(1)}, f32[2,2,4,512,128]{4,3,2,1,0:T(8,128)}, s32[2,16]{1,0:T...) while((s32[]{:T(128)}, f32[2,2,4,512]{3,2,1,0:T(4,128)S(1)}, ...), condition=%wide.region_11.12_spmd, body=%wide.region_3.11_spmd.sunk | while | flops 2204700672 | bytes 64532936 | solution.py:117
  514.2 17.9 %conditional.2 = (f32[2,2,4,512]{3,2,1,0:T(4,128)S(1)}, f32[2,2,4,512]{3,2,1,0:T(4,128)S(1)}, f32[2,2,4,512,128]{4,3,2,1,0:T(8,128)}) conditional(s32[]{:T(128)} %convert_element_type.85, (s32[2,512]{1,0:T(2,128)S(1)}, s32[2,512]{1,0:T(2,128)S(1)}, s32[]{:T(128)}, bf16[2,4096,2,128]{3,1,2,0:T(8,128)(2,1)}, bf16[2,2,4,512,128]{4,3,2,1,0:T(8,128)(2,1)}, ...), branch_computations={%region_7.9_spmd, %region_10.10_spmd} | conditional | flops 2204647424 | bytes 64430148 | solution.py:113
  514.6 4.7 fusion
  519.3 4.1 fusion.2
  523.5 8.7 %multiply_add_fusion = f32[2,2,4,512,128]{4,3,2,1,0:T(8,128)} fusion(f32[2,2,4,512,128]{4,3,2,1,0:T(8,128)} %get-tuple-element.360, f32[2,2,4,512]{3,2,1,0:T(4,128)S(1)} %bitcast.76, f32[2,2,512,4,512]{4,2,3,1,0:T(8,128)S(1)} %get-tuple-element.437, f32[2,2,4,512]{3,2,1,0:T(4,128)S(1)} %max.5, pred[2,512,512]{1,2,0:T(8,128)(4,1)S(1)} %broadcast_compare_fusion, ...), kind=kOutput, calls=%fused_computation.7 | convolution fusion | flops 1096810496 | bytes 26279940 | tf_op jit(solution)/shard_map/while/body/eval_jaxpr/cond/branch_0_fun/shgqk,skhd->shgqd/dot_general | solution.py:105
  533.8 17.9 %conditional.2 = (f32[2,2,4,512]{3,2,1,0:T(4,128)S(1)}, f32[2,2,4,512]{3,2,1,0:T(4,128)S(1)}, f32[2,2,4,512,128]{4,3,2,1,0:T(8,128)}) conditional(s32[]{:T(128)} %convert_element_type.85, (s32[2,512]{1,0:T(2,128)S(1)}, s32[2,512]{1,0:T(2,128)S(1)}, s32[]{:T(128)}, bf16[2,4096,2,128]{3,1,2,0:T(8,128)(2,1)}, bf16[2,2,4,512,128]{4,3,2,1,0:T(8,128)(2,1)}, ...), branch_computations={%region_7.9_spmd, %region_10.10_spmd} | conditional | flops 2204647424 | bytes 64430148 | solution.py:113
  534.2 4.7 fusion
  538.9 4.1 fusion.2
  543.0 8.7 %multiply_add_fusion = f32[2,2,4,512,128]{4,3,2,1,0:T(8,128)} fusion(f32[2,2,4,512,128]{4,3,2,1,0:T(8,128)} %get-tuple-element.360, f32[2,2,4,512]{3,2,1,0:T(4,128)S(1)} %bitcast.76, f32[2,2,512,4,512]{4,2,3,1,0:T(8,128)S(1)} %get-tuple-element.437, f32[2,2,4,512]{3,2,1,0:T(4,128)S(1)} %max.5, pred[2,512,512]{1,2,0:T(8,128)(4,1)S(1)} %broadcast_compare_fusion, ...), kind=kOutput, calls=%fused_computation.7 | convolution fusion | flops 1096810496 | bytes 26279940 | tf_op jit(solution)/shard_map/while/body/eval_jaxpr/cond/branch_0_fun/shgqk,skhd->shgqd/dot_general | solution.py:105
  553.3 17.9 %conditional.2 = (f32[2,2,4,512]{3,2,1,0:T(4,128)S(1)}, f32[2,2,4,512]{3,2,1,0:T(4,128)S(1)}, f32[2,2,4,512,128]{4,3,2,1,0:T(8,128)}) conditional(s32[]{:T(128)} %convert_element_type.85, (s32[2,512]{1,0:T(2,128)S(1)}, s32[2,512]{1,0:T(2,128)S(1)}, s32[]{:T(128)}, bf16[2,4096,2,128]{3,1,2,0:T(8,128)(2,1)}, bf16[2,2,4,512,128]{4,3,2,1,0:T(8,128)(2,1)}, ...), branch_computations={%region_7.9_spmd, %region_10.10_spmd} | conditional | flops 2204647424 | bytes 64430148 | solution.py:113
  553.7 4.7 fusion
  558.4 4.1 fusion.2
  562.5 8.7 %multiply_add_fusion = f32[2,2,4,512,128]{4,3,2,1,0:T(8,128)} fusion(f32[2,2,4,512,128]{4,3,2,1,0:T(8,128)} %get-tuple-element.360, f32[2,2,4,512]{3,2,1,0:T(4,128)S(1)} %bitcast.76, f32[2,2,512,4,512]{4,2,3,1,0:T(8,128)S(1)} %get-tuple-element.437, f32[2,2,4,512]{3,2,1,0:T(4,128)S(1)} %max.5, pred[2,512,512]{1,2,0:T(8,128)(4,1)S(1)} %broadcast_compare_fusion, ...), kind=kOutput, calls=%fused_computation.7 | convolution fusion | flops 1096810496 | bytes 26279940 | tf_op jit(solution)/shard_map/while/body/eval_jaxpr/cond/branch_0_fun/shgqk,skhd->shgqd/dot_general | solution.py:105
  572.8 17.9 %conditional.2 = (f32[2,2,4,512]{3,2,1,0:T(4,128)S(1)}, f32[2,2,4,512]{3,2,1,0:T(4,128)S(1)}, f32[2,2,4,512,128]{4,3,2,1,0:T(8,128)}) conditional(s32[]{:T(128)} %convert_element_type.85, (s32[2,512]{1,0:T(2,128)S(1)}, s32[2,512]{1,0:T(2,128)S(1)}, s32[]{:T(128)}, bf16[2,4096,2,128]{3,1,2,0:T(8,128)(2,1)}, bf16[2,2,4,512,128]{4,3,2,1,0:T(8,128)(2,1)}, ...), branch_computations={%region_7.9_spmd, %region_10.10_spmd} | conditional | flops 2204647424 | bytes 64430148 | solution.py:113
  573.2 4.7 fusion
  577.9 4.1 fusion.2
  582.0 8.7 %multiply_add_fusion = f32[2,2,4,512,128]{4,3,2,1,0:T(8,128)} fusion(f32[2,2,4,512,128]{4,3,2,1,0:T(8,128)} %get-tuple-element.360, f32[2,2,4,512]{3,2,1,0:T(4,128)S(1)} %bitcast.76, f32[2,2,512,4,512]{4,2,3,1,0:T(8,128)S(1)} %get-tuple-element.437, f32[2,2,4,512]{3,2,1,0:T(4,128)S(1)} %max.5, pred[2,512,512]{1,2,0:T(8,128)(4,1)S(1)} %broadcast_compare_fusion, ...), kind=kOutput, calls=%fused_computation.7 | convolution fusion | flops 1096810496 | bytes 26279940 | tf_op jit(solution)/shard_map/while/body/eval_jaxpr/cond/branch_0_fun/shgqk,skhd->shgqd/dot_general | solution.py:105
  592.3 17.9 %conditional.2 = (f32[2,2,4,512]{3,2,1,0:T(4,128)S(1)}, f32[2,2,4,512]{3,2,1,0:T(4,128)S(1)}, f32[2,2,4,512,128]{4,3,2,1,0:T(8,128)}) conditional(s32[]{:T(128)} %convert_element_type.85, (s32[2,512]{1,0:T(2,128)S(1)}, s32[2,512]{1,0:T(2,128)S(1)}, s32[]{:T(128)}, bf16[2,4096,2,128]{3,1,2,0:T(8,128)(2,1)}, bf16[2,2,4,512,128]{4,3,2,1,0:T(8,128)(2,1)}, ...), branch_computations={%region_7.9_spmd, %region_10.10_spmd} | conditional | flops 2204647424 | bytes 64430148 | solution.py:113
  592.7 4.8 fusion
  597.5 4.1 fusion.2
  601.7 8.6 multiply_add_fusion
  611.9 17.8 %conditional.2 = (f32[2,2,4,512]{3,2,1,0:T(4,128)S(1)}, f32[2,2,4,512]{3,2,1,0:T(4,128)S(1)}, f32[2,2,4,512,128]{4,3,2,1,0:T(8,128)}) conditional(s32[]{:T(128)} %convert_element_type.85, (s32[2,512]{1,0:T(2,128)S(1)}, s32[2,512]{1,0:T(2,128)S(1)}, s32[]{:T(128)}, bf16[2,4096,2,128]{3,1,2,0:T(8,128)(2,1)}, bf16[2,2,4,512,128]{4,3,2,1,0:T(8,128)(2,1)}, ...), branch_computations={%region_7.9_spmd, %region_10.10_spmd} | conditional | flops 2204647424 | bytes 64430148 | solution.py:113
  612.3 4.7 fusion
  617.0 4.1 fusion.2
  621.1 8.6 multiply_add_fusion
  631.4 17.8 %conditional.2 = (f32[2,2,4,512]{3,2,1,0:T(4,128)S(1)}, f32[2,2,4,512]{3,2,1,0:T(4,128)S(1)}, f32[2,2,4,512,128]{4,3,2,1,0:T(8,128)}) conditional(s32[]{:T(128)} %convert_element_type.85, (s32[2,512]{1,0:T(2,128)S(1)}, s32[2,512]{1,0:T(2,128)S(1)}, s32[]{:T(128)}, bf16[2,4096,2,128]{3,1,2,0:T(8,128)(2,1)}, bf16[2,2,4,512,128]{4,3,2,1,0:T(8,128)(2,1)}, ...), branch_computations={%region_7.9_spmd, %region_10.10_spmd} | conditional | flops 2204647424 | bytes 64430148 | solution.py:113
  631.7 4.7 fusion
  636.5 4.1 fusion.2
  640.6 8.6 multiply_add_fusion
  650.8 17.9 %conditional.2 = (f32[2,2,4,512]{3,2,1,0:T(4,128)S(1)}, f32[2,2,4,512]{3,2,1,0:T(4,128)S(1)}, f32[2,2,4,512,128]{4,3,2,1,0:T(8,128)}) conditional(s32[]{:T(128)} %convert_element_type.85, (s32[2,512]{1,0:T(2,128)S(1)}, s32[2,512]{1,0:T(2,128)S(1)}, s32[]{:T(128)}, bf16[2,4096,2,128]{3,1,2,0:T(8,128)(2,1)}, bf16[2,2,4,512,128]{4,3,2,1,0:T(8,128)(2,1)}, ...), branch_computations={%region_7.9_spmd, %region_10.10_spmd} | conditional | flops 2204647424 | bytes 64430148 | solution.py:113
  651.2 4.7 fusion
  655.9 4.1 fusion.2
  660.0 8.7 %multiply_add_fusion = f32[2,2,4,512,128]{4,3,2,1,0:T(8,128)} fusion(f32[2,2,4,512,128]{4,3,2,1,0:T(8,128)} %get-tuple-element.360, f32[2,2,4,512]{3,2,1,0:T(4,128)S(1)} %bitcast.76, f32[2,2,512,4,512]{4,2,3,1,0:T(8,128)S(1)} %get-tuple-element.437, f32[2,2,4,512]{3,2,1,0:T(4,128)S(1)} %max.5, pred[2,512,512]{1,2,0:T(8,128)(4,1)S(1)} %broadcast_compare_fusion, ...), kind=kOutput, calls=%fused_computation.7 | convolution fusion | flops 1096810496 | bytes 26279940 | tf_op jit(solution)/shard_map/while/body/eval_jaxpr/cond/branch_0_fun/shgqk,skhd->shgqd/dot_general | solution.py:105
  676.1 26.4 %convolution_convert_fusion = bf16[1024,8192]{1,0:T(8,128)(2,1)} fusion(bf16[1024,1024]{1,0:T(8,128)(2,1)} %reshape.213, bf16[1024,8192]{1,0:T(8,128)(2,1)} %all-gather.20.cloned.1.call-done), kind=kOutput, calls=%fused_computation.41 | convolution fusion | flops 17188257792 | bytes 35651584 | tf_op jit(solution)/shard_map/dot_general | solution.py:120
  702.6 152.7 %reduce-scatter.2.cloned.1.call-done = bf16[1024,2048]{1,0:T(8,128)(2,1)} async-done(((bf16[1024,8192]{1,0:T(8,128)(2,1)}), bf16[1024,2048]{1,0:T(8,128)(2,1)}) %reduce-scatter.2.cloned.1.call-update) | async-done | bytes 4194320 | tf_op jit(solution)/shard_map/reduce_scatter | solution.py:125
  (116 shorter events, 36.3 us)
Async XLA Ops:
  6.5 2.9 copy-start.1
  6.5 52.0 %all-gather.10.cloned.1.call-start = ((), (), s32[]{:S(2)}) async-start(), calls=%async_computation.2 | async-start | bytes 4718592 | tf_op jit(solution)/shard_map/all_gather | solution.py:62
  7.3 209.3 %all-gather.8.cloned.1.call-start = ((), (), s32[]{:S(2)}) async-start(), calls=%async_computation.1 | async-start | bytes 20971520 | tf_op jit(solution)/shard_map/all_gather | solution.py:50
  8.0 257.0 %all-gather.16.cloned.1.call-start = ((), (), s32[]{:S(2)}) async-start(), calls=%async_computation.5 | async-start | bytes 4718592 | tf_op jit(solution)/shard_map/all_gather | solution.py:63
  8.7 407.7 %all-gather.14.cloned.1.call-start = ((), (), s32[]{:S(2)}) async-start(), calls=%async_computation.4 | async-start | bytes 18874368 | tf_op jit(solution)/shard_map/all_gather | solution.py:61
  9.3 460.5 %all-gather.12.cloned.1.call-start = ((), (), s32[]{:S(2)}) async-start(), calls=%async_computation.3 | async-start | bytes 4718592 | tf_op jit(solution)/shard_map/all_gather | solution.py:80
  64.9 159.1 %copy-start.2 = (f32[8192]{0:T(1024)S(1)}, f32[8192]{0:T(1024)}, u32[]{:S(2)}) copy-start(f32[8192]{0:T(1024)} %param.12) | copy-start | bytes 98308
  216.5 7.5 copy-start
  234.1 276.0 %all-gather.18.cloned.1.call-start = ((), (), s32[]{:S(2)}) async-start(), calls=%async_computation.6 | async-start | bytes 4718592 | tf_op jit(solution)/shard_map/all_gather | solution.py:81
  284.1 392.1 %all-gather.20.cloned.1.call-start = ((), (), s32[]{:S(2)}) async-start(), calls=%async_computation.7 | async-start | bytes 18874368 | tf_op jit(solution)/shard_map/all_gather | solution.py:122
  284.8 570.4 %reduce-scatter.2.cloned.1.call-start = ((), (), s32[]{:S(2)}) async-start(), calls=%async_computation.8 | async-start | bytes 20971520 | tf_op jit(solution)/shard_map/reduce_scatter | solution.py:125
Sparse Core Ops, SparseCore 0:
  8.9 49.5 all-gather.9
  60.4 156.0 all-gather.7
  218.1 46.8 all-gather.15
  266.5 149.8 all-gather.13
  417.9 45.0 all-gather.11
  464.4 45.6 all-gather.17
  511.7 149.8 all-gather.19
  702.7 152.5 reduce-scatter.1
where the time goes:
time: 864 us; the launch traced here: 862 us
  waiting for transfers between devices  552 us (64%)
  matrix products  177 us (20%)
  other arithmetic  62 us (7%)
  local copies, waits for them, and re-layouts  51.1 us (6%)
  between operations  13.6 us (2%)
    reduce_scatter x1, waiting for transfers between devices, per_device(): lax.psum_scatter(terms.astype(jnp.bfloat16), 'tp', scatter_dimension=1, t...  153 us
    all_gather x1, waiting for transfers between devices, per_device(): whole = lax.all_gather(tokens, 'tp', axis=2, tiled=True)  152 us
    all_gather x1, waiting for transfers between devices, per_device(): lax.all_gather(w_query, 'ctx', axis=0, tiled=True)  131 us
    dot_general x8, matrix products, update(): jnp.einsum('shgqk,skhd->shgqd', weights.astype(jnp.bfloat16), value_block...  69.1 us
    all_gather x1, waiting for transfers between devices, per_device(): lax.all_gather(w_key, 'ctx', axis=0, tiled=True)  48 us
    dot_general x3, matrix products, per_device(): jnp.dot(normed, piece, preferred_element_type=jnp.float32)  44.1 us
    dot_general x8, matrix products, update(): jnp.einsum('shgqd,skhd->shgqk', query, key_block, preferred_element_type=...  37.6 us
    dot_general x3, local copies, waits for them, and re-layouts, per_device(): jnp.dot(normed, piece, preferred_element_type=jnp.float32)  34.1 us
  transfers between devices with their start and end apart: 8, of which 6 were waited for; matrix products, arithmetic and copies ran while one was open for 31% of the time, Pallas kernels for 0%

commit v1 on v0

--- a/solution.py
+++ b/solution.py
@@ -47,7 +47,9 @@
     total_rows = sequence_batch * rows_dev
     factor = 1.0 / math.sqrt(head_size)
     rank = lax.axis_index("ctx")
-    whole = lax.all_gather(tokens, "tp", axis=2, tiled=True)
+    whole = jnp.concatenate(
+        lax.all_to_all(jnp.stack([tokens] * lax.axis_size("tp")), "tp", 0, 0), axis=2
+    )
     normed = normalize(whole.reshape(total_rows, whole.shape[2]), norm_gain)
     query_pos = positions_of(span_order, rank * rows_dev, rows_dev, block_rows)
     latest = jnp.max(query_pos, axis=1)

time: 864 us -> 856 us (level)
  waiting for transfers between devices: 552 us -> 503 us
  local copies, waits for them, and re-layouts: 51.1 us -> 80.6 us
    all_gather x1 -> x0, waiting for transfers between devices: 152 us -> none  [per_device(): whole = lax.all_gather(tokens, 'tp', axis=2, tiled=True)]
    all_to_all x0 -> x1, waiting for transfers between devices: none -> 125 us  [per_device(): lax.all_to_all(jnp.stack([tokens] * lax.axis_size('tp')), 'tp', 0, 0)]
    all_gather x1, waiting for transfers between devices: 33.8 us -> 0.01 us  [per_device(): value_piece = lax.all_gather(own_values, 'ctx', axis=1, tiled=True)]
    all_gather x1, waiting for transfers between devices: 30.9 us -> 0.02 us  [per_device(): lax.all_gather(value_weight, 'ctx', axis=0, tiled=True)]
    all_gather x1, waiting for transfers between devices: 0.01 us -> 28.9 us  [per_device(): key_piece = lax.all_gather(turned, 'ctx', axis=1, tiled=True)]
    all_to_all x0 -> x1, local copies, waits for them, and re-layouts: none -> 21.7 us  [per_device(): lax.all_to_all(jnp.stack([tokens] * lax.axis_size('tp')), 'tp', 0, 0)]
    all_gather x1, waiting for transfers between devices: 131 us -> 145 us  [per_device(): lax.all_gather(w_query, 'ctx', axis=0, tiled=True)]
  transfers between devices with their start and end apart: 8 -> 8, of which waited for: 6 -> 5; matrix products, arithmetic and copies ran while one was open for 31% -> 34% of each run, Pallas kernels for 0% -> 0%
where the time goes in v1:
time: 856 us; the launch traced here: 853 us
  waiting for transfers between devices  503 us (59%)
  matrix products  172 us (20%)
  local copies, waits for them, and re-layouts  80.6 us (9%)
  other arithmetic  70.1 us (8%)
  between operations  13.7 us (2%)
    reduce_scatter x1, waiting for transfers between devices, per_device(): lax.psum_scatter(terms.astype(jnp.bfloat16), 'tp', scatter_dimension=1, t...  152 us
    all_gather x1, waiting for transfers between devices, per_device(): lax.all_gather(w_query, 'ctx', axis=0, tiled=True)  145 us
    all_to_all x1, waiting for transfers between devices, per_device(): lax.all_to_all(jnp.stack([tokens] * lax.axis_size('tp')), 'tp', 0, 0)  125 us
    dot_general x8, matrix products, update(): jnp.einsum('shgqk,skhd->shgqd', weights.astype(jnp.bfloat16), value_block...  68.9 us
    all_gather x1, waiting for transfers between devices, per_device(): lax.all_gather(w_key, 'ctx', axis=0, tiled=True)  49.7 us
    dot_general x3, matrix products, per_device(): jnp.dot(normed, piece, preferred_element_type=jnp.float32)  38.8 us
    dot_general x8, matrix products, update(): jnp.einsum('shgqd,skhd->shgqk', query, key_block, preferred_element_type=...  38.1 us
    dot_general x3, local copies, waits for them, and re-layouts, per_device(): jnp.dot(normed, piece, preferred_element_type=jnp.float32)  34.1 us
  transfers between devices with their start and end apart: 8, of which 5 were waited for; matrix products, arithmetic and copies ran while one was open for 34% of the time, Pallas kernels for 0%

profile of v1, /device:TPU:0, one launch (start us, length us, event | category | flops | bytes accessed | tf_op | source)
XLA Modules:
  0.0 853.0 jit_solution(5562048849731492615)
XLA Ops:
  6.5 7.4 stack.2
  14.0 7.1 all-to-all-start
  23.9 49.7 %all-gather.7.cloned.1.call-done = bf16[8192,256]{1,0:T(8,128)(2,1)} async-done(((bf16[1024,256]{1,0:T(8,128)(2,1)}), bf16[8192,256]{1,0:T(8,128)(2,1)}) %all-gather.7.cloned.1.call-update) | async-done | bytes 4194320 | tf_op jit(solution)/shard_map/all_gather | solution.py:64
  73.6 6.3 copy.45
  79.9 125.0 %all-to-all-done = bf16[4,2,512,2048]{3,2,1,0:T(8,128)(2,1)} async-done(((bf16[4,2,512,2048]{3,2,1,0:T(8,128)(2,1)}), bf16[4,2,512,2048]{3,2,1,0:T(8,128)(2,1)}, u32[]{:S(2)}, u32[]{:S(2)}) %all-to-all-start) | async-done | bytes 16777248 | tf_op jit(solution)/shard_map/all_to_all | solution.py:51
  204.9 21.7 %copy.44 = bf16[4,2,512,2048]{2,3,0,1:T(8,128)(2,1)} copy(bf16[4,2,512,2048]{3,2,1,0:T(8,128)(2,1)} %all-to-all-done) | data formatting | bytes 33554432 | tf_op jit(solution)/shard_map/all_to_all | solution.py:51
  226.5 10.5 %fusion.21 = f32[2,512]{1,0:T(2,128)S(1)} fusion(bf16[4,2,512,2048]{2,3,0,1:T(8,128)(2,1)} %copy.44), kind=kLoop, calls=%fused_computation.37 | loop fusion | flops 25164800 | bytes 16781312 | tf_op jit(solution)/shard_map/reduce_sum | solution.py:15
  237.5 4.1 fusion.23
  241.6 6.5 fusion.30
  251.0 6.3 copy.51
  257.3 10.7 %convolution_convert_fusion.1 = bf16[2,512,2,128]{3,1,2,0:T(8,128)(2,1)} fusion(bf16[2,512,8192,1]{1,2,3,0:T(8,128)(2,1)} %bitcast.69, bf16[2,128,8192,1]{2,1,0,3:T(8,128)(2,1)} %bitcast.78), kind=kOutput, calls=%fused_computation.46 | convolution fusion | flops 4295229440 | bytes 21495808 | tf_op jit(solution)/shard_map/dot_general | solution.py:68
  269.0 28.9 %all-gather.9.cloned.1.call-done = bf16[2,4096,2,128]{1,3,2,0:T(8,128)(2,1)} async-done(((bf16[2,512,2,128]{1,3,2,0:T(8,128)(2,1)}), bf16[2,4096,2,128]{1,3,2,0:T(8,128)(2,1)}) %all-gather.9.cloned.1.call-update) | async-done | bytes 4194320 | tf_op jit(solution)/shard_map/all_gather | solution.py:82
  297.9 6.4 copy.53
  304.2 145.0 %all-gather.11.cloned.1.call-done = bf16[8192,1024]{1,0:T(8,128)(2,1)} async-done(((bf16[1024,1024]{1,0:T(8,128)(2,1)}), bf16[8192,1024]{1,0:T(8,128)(2,1)}) %all-gather.11.cloned.1.call-update) | async-done | bytes 16777232 | tf_op jit(solution)/shard_map/all_gather | solution.py:63
  449.3 21.5 %copy.47 = bf16[1024,8192]{1,0:T(8,128)(2,1)} copy(bf16[1024,8192]{0,1:T(8,128)(2,1)} %bitcast.71) | data formatting | bytes 33554432 | tf_op jit(solution)/shard_map/dot_general | solution.py:68
  470.7 21.7 %fusion.31 = f32[2,512,8,128]{1,3,2,0:T(8,128)S(1)} fusion(bf16[2,512,8192,1]{1,2,3,0:T(8,128)(2,1)} %bitcast.70, bf16[8,128,8192,1]{2,1,0,3:T(8,128)(2,1)} %bitcast.72), kind=kOutput, calls=%fused_computation.70 | convolution fusion | flops 17179869184 | bytes 37748736 | tf_op jit(solution)/shard_map/dot_general | solution.py:68
  504.5 156.3 %while.19 = (s32[]{:T(128)}, f32[2,2,4,512]{3,2,1,0:T(4,128)S(1)}, f32[2,2,4,512]{3,2,1,0:T(4,128)S(1)}, f32[2,2,4,512,128]{4,3,2,1,0:T(8,128)}, s32[2,16]{1,0:T...) while((s32[]{:T(128)}, f32[2,2,4,512]{3,2,1,0:T(4,128)S(1)}, ...), condition=%wide.region_11.12_spmd, body=%wide.region_3.11_spmd.sunk | while | flops 2204700672 | bytes 64532936 | solution.py:119
  506.3 18.3 %conditional.2 = (f32[2,2,4,512]{3,2,1,0:T(4,128)S(1)}, f32[2,2,4,512]{3,2,1,0:T(4,128)S(1)}, f32[2,2,4,512,128]{4,3,2,1,0:T(8,128)}) conditional(s32[]{:T(128)} %convert_element_type.101, (s32[2,512]{1,0:T(2,128)S(1)}, s32[2,512]{1,0:T(2,128)S(1)}, s32[]{:T(128)}, bf16[2,4096,2,128]{3,1,2,0:T(8,128)(2,1)}, bf16[2,2,4,512,128]{4,3,2,1,0:T(8,128)(2,1)}, ...), branch_computations={%region_7.9_spmd, %region_10.10_spmd} | conditional | flops 2204647424 | bytes 64430148 | solution.py:115
  506.7 5.1 fusion
  511.8 4.1 fusion.2
  516.0 8.6 %multiply_add_fusion = f32[2,2,4,512,128]{4,3,2,1,0:T(8,128)} fusion(f32[2,2,4,512,128]{4,3,2,1,0:T(8,128)} %get-tuple-element.360, f32[2,2,4,512]{3,2,1,0:T(4,128)S(1)} %bitcast.84, f32[2,2,512,4,512]{4,2,3,1,0:T(8,128)S(1)} %get-tuple-element.457, f32[2,2,4,512]{3,2,1,0:T(4,128)S(1)} %max.5, pred[2,512,512]{1,2,0:T(8,128)(4,1)S(1)} %broadcast_compare_fusion, ...), kind=kOutput, calls=%fused_computation.7 | convolution fusion | flops 1096810496 | bytes 26279940 | tf_op jit(solution)/shard_map/while/body/eval_jaxpr/cond/branch_0_fun/shgqk,skhd->shgqd/dot_general | solution.py:107
  526.2 17.9 %conditional.2 = (f32[2,2,4,512]{3,2,1,0:T(4,128)S(1)}, f32[2,2,4,512]{3,2,1,0:T(4,128)S(1)}, f32[2,2,4,512,128]{4,3,2,1,0:T(8,128)}) conditional(s32[]{:T(128)} %convert_element_type.101, (s32[2,512]{1,0:T(2,128)S(1)}, s32[2,512]{1,0:T(2,128)S(1)}, s32[]{:T(128)}, bf16[2,4096,2,128]{3,1,2,0:T(8,128)(2,1)}, bf16[2,2,4,512,128]{4,3,2,1,0:T(8,128)(2,1)}, ...), branch_computations={%region_7.9_spmd, %region_10.10_spmd} | conditional | flops 2204647424 | bytes 64430148 | solution.py:115
  526.6 4.7 fusion
  531.3 4.1 fusion.2
  535.4 8.6 %multiply_add_fusion = f32[2,2,4,512,128]{4,3,2,1,0:T(8,128)} fusion(f32[2,2,4,512,128]{4,3,2,1,0:T(8,128)} %get-tuple-element.360, f32[2,2,4,512]{3,2,1,0:T(4,128)S(1)} %bitcast.84, f32[2,2,512,4,512]{4,2,3,1,0:T(8,128)S(1)} %get-tuple-element.457, f32[2,2,4,512]{3,2,1,0:T(4,128)S(1)} %max.5, pred[2,512,512]{1,2,0:T(8,128)(4,1)S(1)} %broadcast_compare_fusion, ...), kind=kOutput, calls=%fused_computation.7 | convolution fusion | flops 1096810496 | bytes 26279940 | tf_op jit(solution)/shard_map/while/body/eval_jaxpr/cond/branch_0_fun/shgqk,skhd->shgqd/dot_general | solution.py:107
  545.6 17.9 %conditional.2 = (f32[2,2,4,512]{3,2,1,0:T(4,128)S(1)}, f32[2,2,4,512]{3,2,1,0:T(4,128)S(1)}, f32[2,2,4,512,128]{4,3,2,1,0:T(8,128)}) conditional(s32[]{:T(128)} %convert_element_type.101, (s32[2,512]{1,0:T(2,128)S(1)}, s32[2,512]{1,0:T(2,128)S(1)}, s32[]{:T(128)}, bf16[2,4096,2,128]{3,1,2,0:T(8,128)(2,1)}, bf16[2,2,4,512,128]{4,3,2,1,0:T(8,128)(2,1)}, ...), branch_computations={%region_7.9_spmd, %region_10.10_spmd} | conditional | flops 2204647424 | bytes 64430148 | solution.py:115
  546.0 4.7 fusion
  550.7 4.1 fusion.2
  554.9 8.6 %multiply_add_fusion = f32[2,2,4,512,128]{4,3,2,1,0:T(8,128)} fusion(f32[2,2,4,512,128]{4,3,2,1,0:T(8,128)} %get-tuple-element.360, f32[2,2,4,512]{3,2,1,0:T(4,128)S(1)} %bitcast.84, f32[2,2,512,4,512]{4,2,3,1,0:T(8,128)S(1)} %get-tuple-element.457, f32[2,2,4,512]{3,2,1,0:T(4,128)S(1)} %max.5, pred[2,512,512]{1,2,0:T(8,128)(4,1)S(1)} %broadcast_compare_fusion, ...), kind=kOutput, calls=%fused_computation.7 | convolution fusion | flops 1096810496 | bytes 26279940 | tf_op jit(solution)/shard_map/while/body/eval_jaxpr/cond/branch_0_fun/shgqk,skhd->shgqd/dot_general | solution.py:107
  565.1 17.8 %conditional.2 = (f32[2,2,4,512]{3,2,1,0:T(4,128)S(1)}, f32[2,2,4,512]{3,2,1,0:T(4,128)S(1)}, f32[2,2,4,512,128]{4,3,2,1,0:T(8,128)}) conditional(s32[]{:T(128)} %convert_element_type.101, (s32[2,512]{1,0:T(2,128)S(1)}, s32[2,512]{1,0:T(2,128)S(1)}, s32[]{:T(128)}, bf16[2,4096,2,128]{3,1,2,0:T(8,128)(2,1)}, bf16[2,2,4,512,128]{4,3,2,1,0:T(8,128)(2,1)}, ...), branch_computations={%region_7.9_spmd, %region_10.10_spmd} | conditional | flops 2204647424 | bytes 64430148 | solution.py:115
  565.5 4.7 fusion
  570.2 4.1 fusion.2
  574.3 8.6 %multiply_add_fusion = f32[2,2,4,512,128]{4,3,2,1,0:T(8,128)} fusion(f32[2,2,4,512,128]{4,3,2,1,0:T(8,128)} %get-tuple-element.360, f32[2,2,4,512]{3,2,1,0:T(4,128)S(1)} %bitcast.84, f32[2,2,512,4,512]{4,2,3,1,0:T(8,128)S(1)} %get-tuple-element.457, f32[2,2,4,512]{3,2,1,0:T(4,128)S(1)} %max.5, pred[2,512,512]{1,2,0:T(8,128)(4,1)S(1)} %broadcast_compare_fusion, ...), kind=kOutput, calls=%fused_computation.7 | convolution fusion | flops 1096810496 | bytes 26279940 | tf_op jit(solution)/shard_map/while/body/eval_jaxpr/cond/branch_0_fun/shgqk,skhd->shgqd/dot_general | solution.py:107
  584.5 17.8 %conditional.2 = (f32[2,2,4,512]{3,2,1,0:T(4,128)S(1)}, f32[2,2,4,512]{3,2,1,0:T(4,128)S(1)}, f32[2,2,4,512,128]{4,3,2,1,0:T(8,128)}) conditional(s32[]{:T(128)} %convert_element_type.101, (s32[2,512]{1,0:T(2,128)S(1)}, s32[2,512]{1,0:T(2,128)S(1)}, s32[]{:T(128)}, bf16[2,4096,2,128]{3,1,2,0:T(8,128)(2,1)}, bf16[2,2,4,512,128]{4,3,2,1,0:T(8,128)(2,1)}, ...), branch_computations={%region_7.9_spmd, %region_10.10_spmd} | conditional | flops 2204647424 | bytes 64430148 | solution.py:115
  584.9 4.7 fusion
  589.6 4.1 fusion.2
  593.8 8.6 %multiply_add_fusion = f32[2,2,4,512,128]{4,3,2,1,0:T(8,128)} fusion(f32[2,2,4,512,128]{4,3,2,1,0:T(8,128)} %get-tuple-element.360, f32[2,2,4,512]{3,2,1,0:T(4,128)S(1)} %bitcast.84, f32[2,2,512,4,512]{4,2,3,1,0:T(8,128)S(1)} %get-tuple-element.457, f32[2,2,4,512]{3,2,1,0:T(4,128)S(1)} %max.5, pred[2,512,512]{1,2,0:T(8,128)(4,1)S(1)} %broadcast_compare_fusion, ...), kind=kOutput, calls=%fused_computation.7 | convolution fusion | flops 1096810496 | bytes 26279940 | tf_op jit(solution)/shard_map/while/body/eval_jaxpr/cond/branch_0_fun/shgqk,skhd->shgqd/dot_general | solution.py:107
  604.0 17.9 %conditional.2 = (f32[2,2,4,512]{3,2,1,0:T(4,128)S(1)}, f32[2,2,4,512]{3,2,1,0:T(4,128)S(1)}, f32[2,2,4,512,128]{4,3,2,1,0:T(8,128)}) conditional(s32[]{:T(128)} %convert_element_type.101, (s32[2,512]{1,0:T(2,128)S(1)}, s32[2,512]{1,0:T(2,128)S(1)}, s32[]{:T(128)}, bf16[2,4096,2,128]{3,1,2,0:T(8,128)(2,1)}, bf16[2,2,4,512,128]{4,3,2,1,0:T(8,128)(2,1)}, ...), branch_computations={%region_7.9_spmd, %region_10.10_spmd} | conditional | flops 2204647424 | bytes 64430148 | solution.py:115
  604.3 4.8 fusion
  613.2 8.6 %multiply_add_fusion = f32[2,2,4,512,128]{4,3,2,1,0:T(8,128)} fusion(f32[2,2,4,512,128]{4,3,2,1,0:T(8,128)} %get-tuple-element.360, f32[2,2,4,512]{3,2,1,0:T(4,128)S(1)} %bitcast.84, f32[2,2,512,4,512]{4,2,3,1,0:T(8,128)S(1)} %get-tuple-element.457, f32[2,2,4,512]{3,2,1,0:T(4,128)S(1)} %max.5, pred[2,512,512]{1,2,0:T(8,128)(4,1)S(1)} %broadcast_compare_fusion, ...), kind=kOutput, calls=%fused_computation.7 | convolution fusion | flops 1096810496 | bytes 26279940 | tf_op jit(solution)/shard_map/while/body/eval_jaxpr/cond/branch_0_fun/shgqk,skhd->shgqd/dot_general | solution.py:107
  623.4 17.9 %conditional.2 = (f32[2,2,4,512]{3,2,1,0:T(4,128)S(1)}, f32[2,2,4,512]{3,2,1,0:T(4,128)S(1)}, f32[2,2,4,512,128]{4,3,2,1,0:T(8,128)}) conditional(s32[]{:T(128)} %convert_element_type.101, (s32[2,512]{1,0:T(2,128)S(1)}, s32[2,512]{1,0:T(2,128)S(1)}, s32[]{:T(128)}, bf16[2,4096,2,128]{3,1,2,0:T(8,128)(2,1)}, bf16[2,2,4,512,128]{4,3,2,1,0:T(8,128)(2,1)}, ...), branch_computations={%region_7.9_spmd, %region_10.10_spmd} | conditional | flops 2204647424 | bytes 64430148 | solution.py:115
  623.8 4.7 fusion
  632.7 8.6 %multiply_add_fusion = f32[2,2,4,512,128]{4,3,2,1,0:T(8,128)} fusion(f32[2,2,4,512,128]{4,3,2,1,0:T(8,128)} %get-tuple-element.360, f32[2,2,4,512]{3,2,1,0:T(4,128)S(1)} %bitcast.84, f32[2,2,512,4,512]{4,2,3,1,0:T(8,128)S(1)} %get-tuple-element.457, f32[2,2,4,512]{3,2,1,0:T(4,128)S(1)} %max.5, pred[2,512,512]{1,2,0:T(8,128)(4,1)S(1)} %broadcast_compare_fusion, ...), kind=kOutput, calls=%fused_computation.7 | convolution fusion | flops 1096810496 | bytes 26279940 | tf_op jit(solution)/shard_map/while/body/eval_jaxpr/cond/branch_0_fun/shgqk,skhd->shgqd/dot_general | solution.py:107
  642.9 17.8 %conditional.2 = (f32[2,2,4,512]{3,2,1,0:T(4,128)S(1)}, f32[2,2,4,512]{3,2,1,0:T(4,128)S(1)}, f32[2,2,4,512,128]{4,3,2,1,0:T(8,128)}) conditional(s32[]{:T(128)} %convert_element_type.101, (s32[2,512]{1,0:T(2,128)S(1)}, s32[2,512]{1,0:T(2,128)S(1)}, s32[]{:T(128)}, bf16[2,4096,2,128]{3,1,2,0:T(8,128)(2,1)}, bf16[2,2,4,512,128]{4,3,2,1,0:T(8,128)(2,1)}, ...), branch_computations={%region_7.9_spmd, %region_10.10_spmd} | conditional | flops 2204647424 | bytes 64430148 | solution.py:115
  643.3 4.7 fusion
  652.1 8.6 %multiply_add_fusion = f32[2,2,4,512,128]{4,3,2,1,0:T(8,128)} fusion(f32[2,2,4,512,128]{4,3,2,1,0:T(8,128)} %get-tuple-element.360, f32[2,2,4,512]{3,2,1,0:T(4,128)S(1)} %bitcast.84, f32[2,2,512,4,512]{4,2,3,1,0:T(8,128)S(1)} %get-tuple-element.457, f32[2,2,4,512]{3,2,1,0:T(4,128)S(1)} %max.5, pred[2,512,512]{1,2,0:T(8,128)(4,1)S(1)} %broadcast_compare_fusion, ...), kind=kOutput, calls=%fused_computation.7 | convolution fusion | flops 1096810496 | bytes 26279940 | tf_op jit(solution)/shard_map/while/body/eval_jaxpr/cond/branch_0_fun/shgqk,skhd->shgqd/dot_general | solution.py:107
  667.9 26.4 %convolution_convert_fusion = bf16[1024,8192]{1,0:T(8,128)(2,1)} fusion(bf16[1024,1024]{1,0:T(8,128)(2,1)} %reshape.240, bf16[1024,8192]{1,0:T(8,128)(2,1)} %all-gather.17.cloned.1.call-done), kind=kOutput, calls=%fused_computation.40 | convolution fusion | flops 17188257792 | bytes 35651584 | tf_op jit(solution)/shard_map/dot_general | solution.py:122
  694.4 151.8 %reduce-scatter.2.cloned.1.call-done = bf16[1024,2048]{1,0:T(8,128)(2,1)} async-done(((bf16[1024,8192]{1,0:T(8,128)(2,1)}), bf16[1024,2048]{1,0:T(8,128)(2,1)}) %reduce-scatter.2.cloned.1.call-update) | async-done | bytes 4194320 | tf_op jit(solution)/shard_map/reduce_scatter | solution.py:127
  (127 shorter events, 49.1 us)
Async XLA Ops:
  14.0 8.7 %copy-start.6 = (f32[8192]{0:T(1024)S(1)}, f32[8192]{0:T(1024)}, u32[]{:S(2)}) copy-start(f32[8192]{0:T(1024)} %param.12) | copy-start | bytes 98308
  14.0 8.8 %copy-start.5 = (s32[2,16]{1,0:T(2,128)S(1)}, s32[2,16]{1,0:T(2,128)}, u32[]{:S(2)}) copy-start(s32[2,16]{1,0:T(2,128)} %param.13) | copy-start | bytes 388
  14.0 190.9 %all-to-all-start = ((bf16[4,2,512,2048]{3,2,1,0:T(8,128)(2,1)}), bf16[4,2,512,2048]{3,2,1,0:T(8,128)(2,1)}, u32[]{:S(2)}, u32[]{:S(2)}) async-start(bf16[4,2,512,2048]{3,2,1,0:T(8,128)(2,1)} %stack.2), calls=%async_computation | async-start | bytes 33554432 | tf_op jit(solution)/shard_map/all_to_all | solution.py:51
  21.1 52.5 %all-gather.7.cloned.1.call-start = ((), (), s32[]{:S(2)}) async-start(), calls=%async_computation.2 | async-start | bytes 4718592 | tf_op jit(solution)/shard_map/all_gather | solution.py:64
  21.9 229.1 %all-gather.13.cloned.1.call-start = ((), (), s32[]{:S(2)}) async-start(), calls=%async_computation.5 | async-start | bytes 4718592 | tf_op jit(solution)/shard_map/all_gather | solution.py:65
  22.6 275.3 %all-gather.9.cloned.1.call-start = ((), (), s32[]{:S(2)}) async-start(), calls=%async_computation.3 | async-start | bytes 4718592 | tf_op jit(solution)/shard_map/all_gather | solution.py:82
  23.9 224.2 %copy-start.3 = (f32[2,512,64]{1,2,0:T(8,128)}, f32[2,512,64]{1,2,0:T(8,128)S(1)}, u32[]{:S(2)}) copy-start(f32[2,512,64]{1,2,0:T(8,128)S(1)} %get-tuple-element.465) | copy-start | bytes 786436
  226.5 10.9 %copy-start = (bf16[4,2,512,2048]{2,3,0,1:T(8,128)(2,1)S(1)}, bf16[4,2,512,2048]{2,3,0,1:T(8,128)(2,1)}, u32[]{:S(2)}) copy-start(bf16[4,2,512,2048]{2,3,0,1:T(8,128)(2,1)} %copy.44) | copy-start | bytes 50331652
  237.5 4.2 copy-start.2
  241.6 6.5 copy-start.1
  250.4 198.9 %all-gather.11.cloned.1.call-start = ((), (), s32[]{:S(2)}) async-start(), calls=%async_computation.4 | async-start | bytes 18874368 | tf_op jit(solution)/shard_map/all_gather | solution.py:63
  250.9 251.0 %all-gather.15.cloned.1.call-start = ((), (), s32[]{:S(2)}) async-start(), calls=%async_computation.6 | async-start | bytes 4718592 | tf_op jit(solution)/shard_map/all_gather | solution.py:83
  268.0 399.9 %all-gather.17.cloned.1.call-start = ((), (), s32[]{:S(2)}) async-start(), calls=%async_computation.7 | async-start | bytes 18874368 | tf_op jit(solution)/shard_map/all_gather | solution.py:124
  268.6 577.6 %reduce-scatter.2.cloned.1.call-start = ((), (), s32[]{:S(2)}) async-start(), calls=%async_computation.8 | async-start | bytes 20971520 | tf_op jit(solution)/shard_map/reduce_scatter | solution.py:127
  470.7 21.7 %copy-start.4 = (f32[2,512,64]{1,2,0:T(8,128)S(1)}, f32[2,512,64]{1,2,0:T(8,128)}, u32[]{:S(2)}) copy-start(f32[2,512,64]{1,2,0:T(8,128)} %copy-done.3) | copy-start | bytes 786436
Sparse Core Ops, SparseCore 0:
  23.5 49.9 all-gather.6
  75.2 45.6 all-gather.12
  250.5 47.3 all-gather.8
  299.3 149.8 all-gather.10
  450.7 45.0 all-gather.14
  497.3 149.8 all-gather.16
  694.5 151.6 reduce-scatter.1
